TPU v7x, 512 devices: a whole 4x4x16 slice. The times are simulated.
512 devices in a mesh: cand: 16 (over y, z_hi, core), hid: 32 (over z_lo, x).
Axes of the slice: x: 4, y: 4, z: 16 (z_hi: 2, z_lo: 8; z = z_hi * 8 + z_lo), core: 2. Of those that a mesh axis runs over, the one named last changes fastest.
Arguments:
- tokens: bfloat16 [16, 256, 2048], P('cand', None, 'hid'), may hold values from -6 to 6
- cotangent: bfloat16 [16, 256, 2048], P('cand', None, 'hid'), may hold values from -6 to 6
- gate_weight: bfloat16 [2048, 8192], P('cand', 'hid'), may hold values from -0.125 to 0.125
- up_weight: bfloat16 [2048, 8192], P('cand', 'hid'), may hold values from -0.125 to 0.125
- down_weight: bfloat16 [8192, 2048], P('hid', 'cand'), may hold values from -0.125 to 0.125
- width_steps: int32 [16], P('cand'), may hold values from 1 to 8
- block_order: int32 [32], replicated, may hold values from 0 to 31, each once
Outputs:
- grad_tokens: float32 [16, 256, 2048], P('cand', None, 'hid')
- grad_gate: float32 [2048, 8192], P('cand', 'hid')
- grad_up: float32 [2048, 8192], P('cand', 'hid')
- grad_down: float32 [8192, 2048], P('hid', 'cand')
Inputs may be any that keep to these rules, and one draw needn't show every extreme that they name: Candidate c uses the first width_steps[c] * 1024 logical hidden units. `block_order`: names each of the 32 logical blocks once.
All inputs are finite; a program needn't handle non-finite values.
Results may differ from a plain program's by a relative error of at most 0.02.
Values may be sent and summed in bfloat16 or wider, within the bound.
No kernel may reach another device: no remote copies, remote signals or barrier semaphores. Data moves between devices by JAX's collectives and lax.ppermute only.
A program may use at most 64 MiB of HBM per device.

v0:
```python
import jax
import jax.numpy as jnp
from jax import lax
from jax.sharding import PartitionSpec as P

FF = 8192


def gather_turned(arrays, axis, dims):
    turned = [jnp.moveaxis(a, dim, 0) for a, dim in zip(arrays, dims)]
    widths = [t[0].size for t in turned]
    both = jnp.concatenate([t.reshape(-1, w) for t, w in zip(turned, widths)], axis=1)
    filled = lax.all_gather(both, axis, axis=0, tiled=True)
    pieces = jnp.split(filled, [sum(widths[:k]) for k in range(1, len(widths))], axis=1)
    return tuple(
        (
            jnp.moveaxis(b.reshape(-1, *t.shape[1:]), 0, dim)
            for b, t, dim in zip(pieces, turned, dims)
        )
    )


def in_one_piece(arrays, axis, dim, along):
    ends, at = ([], 0)
    for a in arrays[:-1]:
        at += a.shape[along]
        ends.append(at)
    both = jnp.concatenate(arrays, axis=along)
    return tuple(jnp.split(lax.all_gather(both, axis, axis=dim, tiled=True), ends, axis=along))


def copy_for_each(shard, axis):
    size = lax.axis_size(axis)
    return lax.all_to_all(
        jnp.broadcast_to(shard[None], (size, *shard.shape)), axis, 0, 0, tiled=True
    )


def joined_along(pieces, dim):
    shape = list(pieces.shape[1:])
    shape[dim] *= pieces.shape[0]
    return jnp.moveaxis(pieces, 0, dim).reshape(shape)


def gathered_copies(shard, axis, dim):
    pieces = copy_for_each(shard, axis)
    return joined_along(pieces, dim)


def split_up(shard, dim, size):
    shape = shard.shape
    pieces = shard.reshape(*shape[:dim], size, shape[dim] // size, *shape[dim + 1 :])
    return jnp.moveaxis(pieces, dim, 0)


def summed_on_arrival(shard, axis, dim):
    size = lax.axis_size(axis)
    pieces = lax.all_to_all(split_up(shard, dim, size), axis, 0, 0, tiled=True)
    return jnp.sum(pieces.astype(jnp.float32), axis=0)


def in_one_piece_2(arrays, axis, dim, along):
    ends, at = ([], 0)
    for a in arrays[:-1]:
        at += a.shape[along]
        ends.append(at)
    both = jnp.concatenate(arrays, axis=along)
    return tuple(
        jnp.split(lax.psum_scatter(both, axis, scatter_dimension=dim, tiled=True), ends, axis=along)
    )


def shards(tokens, cotangent, gate_weight, up_weight, down_weight, width_steps, block_order):
    inputs, upstream = gather_turned((tokens, cotangent), "hid", (2, 2))
    inputs = inputs[0]
    upstream = upstream[0]
    gate_full, up_full = in_one_piece((gate_weight, up_weight), "cand", 0, 1)
    down_full = gathered_copies(down_weight, "cand", 1)
    width = gate_weight.shape[1]
    places = jnp.arange(block_order.shape[0], dtype=jnp.int32)
    logical = jnp.sum(jnp.where(places == lax.axis_index("hid"), block_order, 0))
    active = logical * width < width_steps[0] * (FF // 8)
    keep = active.astype(jnp.float32)
    gate = jnp.dot(inputs, gate_full, preferred_element_type=jnp.float32)
    up = jnp.dot(inputs, up_full, preferred_element_type=jnp.float32)
    sig = jax.nn.sigmoid(gate)
    act = keep * gate * sig
    hidden = (act * up).astype(jnp.bfloat16)
    dhid = keep * jnp.einsum("td,fd->tf", upstream, down_full, preferred_element_type=jnp.float32)
    forward_d_up = (dhid * act).astype(jnp.bfloat16)
    forward_d_gate = (dhid * up * keep * sig * (1.0 + gate * (1.0 - sig))).astype(jnp.bfloat16)
    down_local = jnp.einsum("tf,td->fd", hidden, upstream, preferred_element_type=jnp.float32)
    down_local, d_gate, d_up = (down_local, forward_d_gate, forward_d_up)
    gate_local = jnp.einsum("td,tf->df", inputs, d_gate, preferred_element_type=jnp.float32)
    up_local = jnp.einsum("td,tf->df", inputs, d_up, preferred_element_type=jnp.float32)
    input_part = jnp.einsum("tf,df->td", d_gate, gate_full, preferred_element_type=jnp.float32)
    input_part = input_part + jnp.einsum(
        "tf,df->td", d_up, up_full, preferred_element_type=jnp.float32
    )
    gate_local, up_local, input_part = (gate_local, up_local, input_part)
    grad_tokens = summed_on_arrival(input_part[None].astype(jnp.bfloat16), "hid", 2)
    grad_gate, grad_up = tuple(
        (
            part.astype(jnp.float32)
            for part in in_one_piece_2(
                (gate_local.astype(jnp.bfloat16), up_local.astype(jnp.bfloat16)), "cand", 0, 1
            )
        )
    )
    grad_down = summed_on_arrival(down_local.astype(jnp.bfloat16), "cand", 1)
    return (grad_tokens, grad_gate, grad_up, grad_down)


def solution(mesh):
    in_specs = (
        P("cand", None, "hid"),
        P("cand", None, "hid"),
        P("cand", "hid"),
        P("cand", "hid"),
        P("hid", "cand"),
        P("cand"),
        P(),
    )
    out_specs = (P("cand", None, "hid"), P("cand", "hid"), P("cand", "hid"), P("hid", "cand"))
    return jax.shard_map(shards, mesh=mesh, in_specs=in_specs, out_specs=out_specs, check_vma=False)
```

profile of v0, /device:TPU:2, one launch (start us, length us, event | category | flops | bytes accessed | tf_op | source)
XLA Modules:
  0.0 553.6 jit_solution(2269472352284854888)
XLA Ops:
  7.2 0.0 copy-start.4
  7.2 0.0 all-gather.5.cloned.1.call-start
  7.2 1.5 pad_maximum_fusion.1
  8.8 0.0 all-gather.5.cloned.1.call-update
  8.8 0.0 all-gather.3.cloned.1.call-start
  8.8 1.4 pad_maximum_fusion.2
  10.2 0.0 all-gather.3.cloned.1.call-update
  10.3 0.9 copy.17
  11.2 1.1 broadcast_in_dim.12
  12.3 17.8 %all-to-all-start = ((bf16[16,256,128]{1,2,0:T(8,128)(2,1)}), bf16[16,256,128]{1,2,0:T(8,128)(2,1)S(1)}, u32[]{:S(2)}, u32[]{:S(2)}) async-start(bf16[16,256,128]{1,2,0:T(8,128)(2,1)} %broadcast_in_dim.12), calls=%async_computation | async-start | bytes 2097152 | tf_op jit(solution)/shard_map/all_to_all | solution.py:34
  30.8 0.0 copy-done.4
  30.8 0.6 fusion.9
  32.1 88.1 %all-gather.5.cloned.1.call-done = bf16[2048,512]{1,0:T(8,128)(2,1)} async-done(((bf16[128,512]{1,0:T(8,128)(2,1)}), bf16[2048,512]{1,0:T(8,128)(2,1)}) %all-gather.5.cloned.1.call-update) | async-done | bytes 2097168 | tf_op jit(solution)/shard_map/all_gather | solution.py:29
  120.1 237.6 %all-gather.3.cloned.1.call-done = bf16[2048,512]{1,0:T(8,128)(2,1)} async-done(((bf16[64,512]{1,0:T(8,128)(2,1)}), bf16[2048,512]{1,0:T(8,128)(2,1)}) %all-gather.3.cloned.1.call-update) | async-done | bytes 2097168 | tf_op jit(solution)/shard_map/all_gather | solution.py:13
  357.7 2.2 fusion.4
  359.9 0.1 copy-done
  360.0 1.8 fusion.7
  361.8 0.0 copy-start.6
  361.8 0.5 fusion.1
  362.3 0.0 copy-done.5
  362.3 0.1 copy-done.6
  362.5 1.2 copy.29
  363.7 0.0 all-to-all-done
  363.7 1.0 copy-done.3
  364.7 4.5 all-to-all-start.2
  369.2 0.0 copy-start.2
  369.2 2.0 multiply_convert_fusion.1
  371.2 0.0 copy-done.2
  371.3 0.5 fusion.2
  371.7 0.5 fusion
  372.2 1.3 copy.18
  373.6 2.8 convolution_convert_fusion.1
  376.4 18.0 %all-to-all-done.2 = bf16[16,256,128]{2,1,0:T(8,128)(2,1)S(1)} async-done(((bf16[16,256,128]{2,1,0:T(8,128)(2,1)}), bf16[16,256,128]{2,1,0:T(8,128)(2,1)S(1)}, u32[]{:S(2)}, u32[]{:S(2)}) %all-to-all-start.2) | async-done | bytes 1048608 | tf_op jit(solution)/shard_map/all_to_all | solution.py:58
  394.4 22.8 %all-to-all-start.1 = ((bf16[32,1,256,64]{2,3,1,0:T(8,128)(2,1)}), bf16[32,1,256,64]{2,3,1,0:T(8,128)(2,1)}, u32[]{:S(2)}, u32[]{:S(2)}) async-start(bf16[32,1,256,64]{2,3,1,0:T(8,128)(2,1)} %bitcast.17), calls=%async_computation.1 | async-start | bytes 2097152 | tf_op jit(solution)/shard_map/all_to_all | solution.py:58
  417.1 0.0 reduce-scatter.4.cloned.1.call-start
  417.2 0.5 convolution_convert_fusion.2
  417.7 1.4 pad_maximum_fusion
  419.0 2.5 copy.23
  421.6 0.0 reduce-scatter.4.cloned.1.call-update
  421.6 120.1 %reduce-scatter.4.cloned.1.call-done = bf16[128,512]{1,0:T(8,128)(2,1)} async-done(((bf16[2048,512]{1,0:T(8,128)(2,1)}), bf16[128,512]{1,0:T(8,128)(2,1)}) %reduce-scatter.4.cloned.1.call-update) | async-done | bytes 131088
  541.6 0.9 fusion.11
  542.5 0.1 copy.26
  542.6 0.8 copy.22
  543.4 0.1 copy.25
  543.5 0.8 copy.21
  544.3 0.8 convert_reduce_fusion
  545.1 0.0 all-to-all-done.1
  545.1 2.0 convert_reduce_fusion.1
  (5 shorter events, 0.0 us)
Async XLA Ops:
  7.2 23.6 %copy-start.4 = (s32[32]{0:T(128)S(1)}, s32[32]{0:T(128)}, u32[]{:S(2)}) copy-start(s32[32]{0:T(128)} %param.13) | copy-start | bytes 388
  7.2 113.0 %all-gather.5.cloned.1.call-start = ((), (), s32[]{:S(2)}) async-start(), calls=%async_computation.5 | async-start | bytes 2228224 | tf_op jit(solution)/shard_map/all_gather | solution.py:29
  8.8 349.0 %all-gather.3.cloned.1.call-start = ((), (), s32[]{:S(2)}) async-start(), calls=%async_computation.4 | async-start | bytes 2162688 | tf_op jit(solution)/shard_map/all_gather | solution.py:13
  12.3 351.4 %all-to-all-start = ((bf16[16,256,128]{1,2,0:T(8,128)(2,1)}), bf16[16,256,128]{1,2,0:T(8,128)(2,1)S(1)}, u32[]{:S(2)}, u32[]{:S(2)}) async-start(bf16[16,256,128]{1,2,0:T(8,128)(2,1)} %broadcast_in_dim.12), calls=%async_computation | async-start | bytes 2097152 | tf_op jit(solution)/shard_map/all_to_all | solution.py:34
  357.7 2.2 copy-start
  360.0 2.3 copy-start.5
  361.8 0.7 copy-start.6
  363.7 1.0 copy-start.3
  364.7 29.7 %all-to-all-start.2 = ((bf16[16,256,128]{2,1,0:T(8,128)(2,1)}), bf16[16,256,128]{2,1,0:T(8,128)(2,1)S(1)}, u32[]{:S(2)}, u32[]{:S(2)}) async-start(bf16[16,256,128]{2,1,0:T(8,128)(2,1)} %bitcast.49), calls=%async_computation.2 | async-start | bytes 2097152 | tf_op jit(solution)/shard_map/all_to_all | solution.py:58
  369.2 2.1 copy-start.2
  373.5 43.6 %copy-start.1 = (bf16[2048,512]{1,0:T(8,128)(2,1)S(1)}, bf16[2048,512]{1,0:T(8,128)(2,1)}, u32[]{:S(2)}) copy-start(bf16[2048,512]{1,0:T(8,128)(2,1)} %all-gather.3.cloned.1.call-done) | copy-start | bytes 6291460
  394.4 150.7 %all-to-all-start.1 = ((bf16[32,1,256,64]{2,3,1,0:T(8,128)(2,1)}), bf16[32,1,256,64]{2,3,1,0:T(8,128)(2,1)}, u32[]{:S(2)}, u32[]{:S(2)}) async-start(bf16[32,1,256,64]{2,3,1,0:T(8,128)(2,1)} %bitcast.17), calls=%async_computation.1 | async-start | bytes 2097152 | tf_op jit(solution)/shard_map/all_to_all | solution.py:58
  417.1 124.5 %reduce-scatter.4.cloned.1.call-start = ((), (), s32[]{:S(2)}) async-start(), calls=%async_computation.6 | async-start | bytes 2228224
Sparse Core Ops, SparseCore 0:
  11.8 108.2 all-gather.4
  122.8 234.8 all-gather.2
  422.7 118.8 reduce-scatter.3
where the time goes:
time: 554 us
  waiting for transfers between devices  464 us (84%)
  starting transfers between devices  45.2 us (8%)
  between operations  15.2 us (3%)
  local copies, waits for them, and re-layouts  11 us (2%)
  matrix products  10.7 us (2%)
  other arithmetic  7.75 us (1%)
    all_gather x1, waiting for transfers between devices, gather_turned(): filled = lax.all_gather(both, axis, axis=0, tiled=True)  238 us
    unnamed x4, waiting for transfers between devices  120 us
    all_gather x1, waiting for transfers between devices, in_one_piece(): lax.all_gather(both, axis, axis=dim, tiled=True)  88.1 us
    all_to_all x2, starting transfers between devices, summed_on_arrival(): pieces = lax.all_to_all(split_up(shard, dim, size), axis, 0, 0, tiled=True)  27.2 us
    all_to_all x2, waiting for transfers between devices, summed_on_arrival(): pieces = lax.all_to_all(split_up(shard, dim, size), axis, 0, 0, tiled=True)  18 us
    all_to_all x1, starting transfers between devices, copy_for_each(): lax.all_to_all(jnp.broadcast_to(shard[None], (size, *shard.shape)), axis,...  17.8 us
  transfers between devices with their start and end apart: 6, of which 4 were waited for; matrix products, arithmetic and copies ran while one was open for 4% of the time, Pallas kernels for 0%

commit v1 on v0

--- a/solution.py
+++ b/solution.py
@@ -10,7 +10,9 @@
     turned = [jnp.moveaxis(a, dim, 0) for a, dim in zip(arrays, dims)]
     widths = [t[0].size for t in turned]
     both = jnp.concatenate([t.reshape(-1, w) for t, w in zip(turned, widths)], axis=1)
-    filled = lax.all_gather(both, axis, axis=0, tiled=True)
+    filled = jnp.concatenate(
+        lax.all_to_all(jnp.stack([both] * lax.axis_size(axis)), axis, 0, 0), axis=0
+    )
     pieces = jnp.split(filled, [sum(widths[:k]) for k in range(1, len(widths))], axis=1)
     return tuple(
         (

time: 554 us -> 414 us (0.75)
  waiting for transfers between devices: 464 us -> 324 us
    all_gather x1 -> x0, waiting for transfers between devices: 238 us -> none  [gather_turned(): filled = lax.all_gather(both, axis, axis=0, tiled=True)]
    all_to_all x0 -> x1, waiting for transfers between devices: none -> 123 us  [gather_turned(): lax.all_to_all(jnp.stack([both] * lax.axis_size(axis)), axis, 0, 0)]
    all_gather x1, waiting for transfers between devices: 88.1 us -> 0.02 us  [in_one_piece(): lax.all_gather(both, axis, axis=dim, tiled=True)]
    all_to_all x1, waiting for transfers between devices: 0.01 us -> 45.3 us  [copy_for_each(): lax.all_to_all(jnp.broadcast_to(shard[None], (size, *shard.shape)), axis,...]
    all_to_all x2, waiting for transfers between devices: 18 us -> 35.2 us  [summed_on_arrival(): pieces = lax.all_to_all(split_up(shard, dim, size), axis, 0, 0, tiled=True)]
    all_to_all x0 -> x1, starting transfers between devices: none -> 15.8 us  [gather_turned(): lax.all_to_all(jnp.stack([both] * lax.axis_size(axis)), axis, 0, 0)]
    all_to_all x1, starting transfers between devices: 17.8 us -> 10.3 us  [copy_for_each(): lax.all_to_all(jnp.broadcast_to(shard[None], (size, *shard.shape)), axis,...]
    all_to_all x2, starting transfers between devices: 27.2 us -> 20.1 us  [summed_on_arrival(): pieces = lax.all_to_all(split_up(shard, dim, size), axis, 0, 0, tiled=True)]
  transfers between devices with their start and end apart: 6 -> 6, of which waited for: 4 -> 4; matrix products, arithmetic and copies ran while one was open for 4% -> 5% of each run, Pallas kernels for 0% -> 0%
where the time goes in v1:
time: 414 us; the launch traced here: 413 us
  waiting for transfers between devices  324 us (78%)
  starting transfers between devices  46.2 us (11%)
  between operations  15.5 us (4%)
  local copies, waits for them, and re-layouts  13.4 us (3%)
  matrix products  8.73 us (2%)
  other arithmetic  5.12 us (1%)
    all_to_all x1, waiting for transfers between devices, gather_turned(): lax.all_to_all(jnp.stack([both] * lax.axis_size(axis)), axis, 0, 0)  123 us
    unnamed x3, waiting for transfers between devices  121 us
    all_to_all x1, waiting for transfers between devices, copy_for_each(): lax.all_to_all(jnp.broadcast_to(shard[None], (size, *shard.shape)), axis,...  45.3 us
    all_to_all x2, waiting for transfers between devices, summed_on_arrival(): pieces = lax.all_to_all(split_up(shard, dim, size), axis, 0, 0, tiled=True)  35.2 us
    all_to_all x2, starting transfers between devices, summed_on_arrival(): pieces = lax.all_to_all(split_up(shard, dim, size), axis, 0, 0, tiled=True)  20.1 us
    all_to_all x1, starting transfers between devices, gather_turned(): lax.all_to_all(jnp.stack([both] * lax.axis_size(axis)), axis, 0, 0)  15.8 us
    all_to_all x1, starting transfers between devices, copy_for_each(): lax.all_to_all(jnp.broadcast_to(shard[None], (size, *shard.shape)), axis,...  10.3 us
  transfers between devices with their start and end apart: 6, of which 4 were waited for; matrix products, arithmetic and copies ran while one was open for 5% of the time, Pallas kernels for 0%

profile of v1, /device:TPU:2, one launch (start us, length us, event | category | flops | bytes accessed | tf_op | source)
XLA Modules:
  0.0 413.3 jit_solution(1728546453825842605)
XLA Ops:
  7.2 0.8 pad_maximum_fusion.2
  7.9 1.6 stack.2
  9.5 15.8 %all-to-all-start = ((bf16[32,64,512]{2,1,0:T(8,128)(2,1)}), bf16[32,64,512]{2,1,0:T(8,128)(2,1)S(1)}, u32[]{:S(2)}, u32[]{:S(2)}) async-start(bf16[32,64,512]{2,1,0:T(8,128)(2,1)} %stack.2), calls=%async_computation | async-start | bytes 4194304 | tf_op jit(solution)/shard_map/all_to_all | solution.py:14
  25.3 0.0 copy-start.7
  25.3 0.0 all-gather.2.cloned.1.call-start
  25.4 0.0 copy-done.5
  25.4 0.0 copy-done.6
  25.4 0.7 pad_maximum_fusion.1
  26.1 0.0 all-gather.2.cloned.1.call-update
  26.1 0.1 copy.17
  26.2 122.7 %all-to-all-done = bf16[32,64,512]{2,1,0:T(8,128)(2,1)S(1)} async-done(((bf16[32,64,512]{2,1,0:T(8,128)(2,1)}), bf16[32,64,512]{2,1,0:T(8,128)(2,1)S(1)}, u32[]{:S(2)}, u32[]{:S(2)}) %all-to-all-start) | async-done | bytes 2097184 | tf_op jit(solution)/shard_map/all_to_all | solution.py:14
  148.9 1.1 broadcast_in_dim.12
  150.0 10.3 %all-to-all-start.1 = ((bf16[16,256,128]{1,2,0:T(8,128)(2,1)}), bf16[16,256,128]{1,2,0:T(8,128)(2,1)S(1)}, u32[]{:S(2)}, u32[]{:S(2)}) async-start(bf16[16,256,128]{1,2,0:T(8,128)(2,1)} %broadcast_in_dim.12), calls=%async_computation.1 | async-start | bytes 2097152 | tf_op jit(solution)/shard_map/all_to_all | solution.py:36
  161.0 0.6 fusion.9
  162.3 0.0 all-gather.2.cloned.1.call-done
  162.3 1.8 fusion.4
  164.2 0.0 copy-done.1
  164.2 0.5 fusion.7
  164.7 0.5 fusion.1
  165.2 0.2 copy-done.9
  165.4 1.2 copy.29
  166.6 45.3 %all-to-all-done.1 = bf16[16,256,128]{1,2,0:T(8,128)(2,1)S(1)} async-done(((bf16[16,256,128]{1,2,0:T(8,128)(2,1)}), bf16[16,256,128]{1,2,0:T(8,128)(2,1)S(1)}, u32[]{:S(2)}, u32[]{:S(2)}) %all-to-all-start.1) | async-done | bytes 1048608 | tf_op jit(solution)/shard_map/all_to_all | solution.py:36
  211.9 1.0 copy-done.3
  212.9 8.6 %all-to-all-start.3 = ((bf16[16,256,128]{2,1,0:T(8,128)(2,1)}), bf16[16,256,128]{2,1,0:T(8,128)(2,1)S(1)}, u32[]{:S(2)}, u32[]{:S(2)}) async-start(bf16[16,256,128]{2,1,0:T(8,128)(2,1)} %bitcast.58), calls=%async_computation.3 | async-start | bytes 2097152 | tf_op jit(solution)/shard_map/all_to_all | solution.py:60
  221.5 2.0 multiply_convert_fusion.1
  223.5 0.0 copy-done.2
  223.6 0.5 fusion.2
  224.0 1.5 fusion
  225.5 2.3 copy.18
  227.8 1.5 convolution_convert_fusion.1
  229.2 35.2 %all-to-all-done.3 = bf16[16,256,128]{2,1,0:T(8,128)(2,1)S(1)} async-done(((bf16[16,256,128]{2,1,0:T(8,128)(2,1)}), bf16[16,256,128]{2,1,0:T(8,128)(2,1)S(1)}, u32[]{:S(2)}, u32[]{:S(2)}) %all-to-all-start.3) | async-done | bytes 1048608 | tf_op jit(solution)/shard_map/all_to_all | solution.py:60
  264.4 11.5 %all-to-all-start.2 = ((bf16[32,1,256,64]{2,3,1,0:T(8,128)(2,1)}), bf16[32,1,256,64]{2,3,1,0:T(8,128)(2,1)}, u32[]{:S(2)}, u32[]{:S(2)}) async-start(bf16[32,1,256,64]{2,3,1,0:T(8,128)(2,1)} %bitcast.57), calls=%async_computation.2 | async-start | bytes 2097152 | tf_op jit(solution)/shard_map/all_to_all | solution.py:60
  275.9 0.0 reduce-scatter.4.cloned.1.call-start
  275.9 0.0 copy-start
  275.9 0.5 convolution_convert_fusion.2
  276.4 0.7 copy-done
  277.2 0.2 pad_maximum_fusion
  277.4 2.5 copy.23
  279.9 0.0 reduce-scatter.4.cloned.1.call-update
  280.0 121.0 %reduce-scatter.4.cloned.1.call-done = bf16[128,512]{1,0:T(8,128)(2,1)} async-done(((bf16[2048,512]{1,0:T(8,128)(2,1)}), bf16[128,512]{1,0:T(8,128)(2,1)}) %reduce-scatter.4.cloned.1.call-update) | async-done | bytes 131088
  400.9 0.9 fusion.11
  401.8 0.1 copy.26
  401.9 0.8 copy.22
  402.7 0.1 copy.25
  402.8 0.8 copy.21
  403.6 0.8 convert_reduce_fusion
  404.4 0.0 all-to-all-done.2
  404.4 2.0 convert_reduce_fusion.1
  (11 shorter events, 0.0 us)
Async XLA Ops:
  9.5 15.9 %copy-start.5 = (bf16[128,256]{1,0:T(8,128)(2,1)S(1)}, bf16[128,256]{1,0:T(8,128)(2,1)}, u32[]{:S(2)}) copy-start(bf16[128,256]{1,0:T(8,128)(2,1)} %param.10) | copy-start | bytes 196612
  9.5 15.9 %copy-start.6 = (bf16[128,256]{1,0:T(8,128)(2,1)S(1)}, bf16[128,256]{1,0:T(8,128)(2,1)}, u32[]{:S(2)}) copy-start(bf16[128,256]{1,0:T(8,128)(2,1)} %param.9) | copy-start | bytes 196612
  9.5 16.6 %copy-start.4 = (bf16[256,128]{1,0:T(8,128)(2,1)S(1)}, bf16[256,128]{1,0:T(8,128)(2,1)}, u32[]{:S(2)}) copy-start(bf16[256,128]{1,0:T(8,128)(2,1)} %param.11) | copy-start | bytes 196612
  9.5 139.4 %all-to-all-start = ((bf16[32,64,512]{2,1,0:T(8,128)(2,1)}), bf16[32,64,512]{2,1,0:T(8,128)(2,1)S(1)}, u32[]{:S(2)}, u32[]{:S(2)}) async-start(bf16[32,64,512]{2,1,0:T(8,128)(2,1)} %stack.2), calls=%async_computation | async-start | bytes 4194304 | tf_op jit(solution)/shard_map/all_to_all | solution.py:14
  25.3 135.6 %copy-start.7 = (s32[32]{0:T(128)S(1)}, s32[32]{0:T(128)}, u32[]{:S(2)}) copy-start(s32[32]{0:T(128)} %param.13) | copy-start | bytes 388
  25.3 136.9 %all-gather.2.cloned.1.call-start = ((), (), s32[]{:S(2)}) async-start(), calls=%async_computation.5 | async-start | bytes 2228224 | tf_op jit(solution)/shard_map/all_gather | solution.py:31
  150.0 61.9 %all-to-all-start.1 = ((bf16[16,256,128]{1,2,0:T(8,128)(2,1)}), bf16[16,256,128]{1,2,0:T(8,128)(2,1)S(1)}, u32[]{:S(2)}, u32[]{:S(2)}) async-start(bf16[16,256,128]{1,2,0:T(8,128)(2,1)} %broadcast_in_dim.12), calls=%async_computation.1 | async-start | bytes 2097152 | tf_op jit(solution)/shard_map/all_to_all | solution.py:36
  162.3 1.9 copy-start.1
  164.2 1.0 copy-start.8
  164.7 0.7 copy-start.9
  211.9 1.0 copy-start.3
  212.9 51.5 %all-to-all-start.3 = ((bf16[16,256,128]{2,1,0:T(8,128)(2,1)}), bf16[16,256,128]{2,1,0:T(8,128)(2,1)S(1)}, u32[]{:S(2)}, u32[]{:S(2)}) async-start(bf16[16,256,128]{2,1,0:T(8,128)(2,1)} %bitcast.58), calls=%async_computation.3 | async-start | bytes 2097152 | tf_op jit(solution)/shard_map/all_to_all | solution.py:60
  221.5 2.1 copy-start.2
  264.4 140.0 %all-to-all-start.2 = ((bf16[32,1,256,64]{2,3,1,0:T(8,128)(2,1)}), bf16[32,1,256,64]{2,3,1,0:T(8,128)(2,1)}, u32[]{:S(2)}, u32[]{:S(2)}) async-start(bf16[32,1,256,64]{2,3,1,0:T(8,128)(2,1)} %bitcast.57), calls=%async_computation.2 | async-start | bytes 2097152 | tf_op jit(solution)/shard_map/all_to_all | solution.py:60
  275.9 125.1 %reduce-scatter.4.cloned.1.call-start = ((), (), s32[]{:S(2)}) async-start(), calls=%async_computation.6 | async-start | bytes 2228224
  275.9 1.2 copy-start
Sparse Core Ops, SparseCore 0:
  30.0 98.9 all-gather.1
  281.5 119.3 reduce-scatter.3
